TPU v7x, 32 devices: a whole 2x2x4 slice. The times are simulated.
32 devices in a mesh: frames: 8 (over z, y), heads: 4 (over x, core).
Axes of the slice: x: 2, y: 2, z: 4, core: 2. Of those that a mesh axis runs over, the one named last changes fastest.
Arguments:
- tokens: bfloat16 [1024, 4096], P('frames'), may hold values from -6 to 6
- norm_gain: float32 [4096], replicated, may hold values from 0.5 to 1.5
- w_query: bfloat16 [4096, 2048], P(None, 'heads'), may hold values from -0.09375 to 0.09375
- w_key: bfloat16 [4096, 2048], P(None, 'heads'), may hold values from -0.09375 to 0.09375
- w_value: bfloat16 [4096, 2048], P(None, 'heads'), may hold values from -0.09375 to 0.09375
- head_gain: float32 [2048], P('heads'), may hold values from 0.5 to 1.5
- w_out: bfloat16 [2048, 4096], P('heads'), may hold values from -0.125 to 0.125
Outputs:
- mixed: bfloat16 [1024, 4096], P('frames', 'heads')
All inputs are finite; a program needn't handle non-finite values.
Results may differ from a plain program's by a relative error of at most 0.015.
Values may be sent and summed in bfloat16 or wider, within the bound.
A program may use at most 128 MiB of HBM per device.

v0:
```python
import math

import jax
import jax.numpy as jnp
from jax import lax
from jax.sharding import PartitionSpec as P

HD = 128


epsilon = 1e-06


def folded(x, axis, dim, absorb, carry):
    whole = jax.tree.map(lambda part: lax.all_gather(part, axis, axis=dim, tiled=True), x)
    return absorb(carry, whole, jnp.int32(0))


def block_update(state, query_part, query_start, key_block, value_block, key_start):
    running_max, running_sum, weighted = state
    half_rows = query_part.shape[0]
    inv_root = 1.0 / math.sqrt(query_part.shape[2])
    scores = (
        jnp.einsum("qhd,khd->hqk", query_part, key_block, preferred_element_type=jnp.float32)
        * inv_root
    )
    query_pos = query_start + jnp.arange(half_rows, dtype=jnp.int32)
    key_pos = key_start + jnp.arange(key_block.shape[0], dtype=jnp.int32)
    visible = (key_pos[None, :] <= query_pos[:, None])[None]
    scores = jnp.where(visible, scores, jnp.float32(-1e30))
    top = jnp.maximum(running_max, jnp.max(scores, axis=2))
    expscores = jnp.where(visible, jnp.exp(scores - top[:, :, None]), jnp.float32(0.0))
    shrink = jnp.exp(running_max - top)
    running_sum = running_sum * shrink + jnp.sum(expscores, axis=2)
    weighted = weighted * shrink[:, :, None] + jnp.einsum(
        "hqk,khd->hqd", expscores, value_block.astype(jnp.float32)
    )
    return (top, running_sum, weighted)


def guarded_update(state, query_part, query_start, key_block, value_block, key_start):
    needed = key_start <= query_start + query_part.shape[0] - 1
    return lax.cond(
        needed,
        lambda inner: block_update(
            inner, query_part, query_start, key_block, value_block, key_start
        ),
        lambda inner: inner,
        state,
    )


def per_device(tokens, norm_gain, w_query, w_key, w_value, head_gain, w_out):
    widened = tokens.astype(jnp.float32)
    normed = (
        widened
        * lax.rsqrt(jnp.mean(widened * widened, axis=1, keepdims=True) + epsilon)
        * norm_gain[None, :]
    ).astype(jnp.bfloat16)
    query_rows = jnp.dot(normed, w_query, preferred_element_type=jnp.float32).astype(jnp.bfloat16)
    key_rows = jnp.dot(normed, w_key, preferred_element_type=jnp.float32).astype(jnp.bfloat16)
    value_rows = jnp.dot(normed, w_value, preferred_element_type=jnp.float32).astype(jnp.bfloat16)
    row_count = tokens.shape[0]
    half_rows = row_count // 2
    heads_here = w_query.shape[1] // HD
    my_index = lax.axis_index("frames")
    query_starts = (my_index * row_count, my_index * row_count + half_rows)
    query_three = query_rows.reshape(row_count, heads_here, HD)
    query_parts = (query_three[:half_rows], query_three[half_rows:])
    key_three = key_rows.reshape(row_count, heads_here, HD)
    value_three = value_rows.reshape(row_count, heads_here, HD)

    def accumulate(state_pair, pieces, start):
        key_piece, value_piece = pieces
        block_total = key_piece.shape[0] // half_rows
        key_blocks = key_piece.reshape(block_total, half_rows, heads_here, HD)
        value_blocks = value_piece.reshape(block_total, half_rows, heads_here, HD)
        first_block = start // half_rows

        def advance(inner_pair, packed):
            key_block, value_block, offset_index = packed
            block_index = first_block + offset_index
            key_start = block_index * half_rows
            updated = tuple(
                (
                    guarded_update(
                        inner_pair[half_index],
                        query_parts[half_index],
                        query_starts[half_index],
                        key_block,
                        value_block,
                        key_start,
                    )
                    for half_index in range(2)
                )
            )
            return (updated, None)

        state_pair, unused = lax.scan(
            advance,
            state_pair,
            (key_blocks, value_blocks, jnp.arange(block_total, dtype=jnp.int32)),
        )
        return state_pair

    one_state = (
        jnp.full((heads_here, half_rows), -1e30, jnp.float32),
        jnp.zeros((heads_here, half_rows), jnp.float32),
        jnp.zeros((heads_here, half_rows, HD), jnp.float32),
    )
    final_pair = folded((key_three, value_three), "frames", 0, accumulate, (one_state, one_state))
    attended = jnp.concatenate(
        [
            final_pair[0][2] / final_pair[0][1][:, :, None],
            final_pair[1][2] / final_pair[1][1][:, :, None],
        ],
        axis=1,
    )
    scaled = (
        attended
        * lax.rsqrt(jnp.mean(attended * attended, axis=2, keepdims=True) + epsilon)
        * head_gain.reshape(heads_here, 1, HD)
    )
    headed = (
        jnp.transpose(scaled, (1, 0, 2)).reshape(row_count, heads_here * HD).astype(jnp.bfloat16)
    )
    partial_terms = jnp.dot(headed, w_out, preferred_element_type=jnp.float32)
    return (
        lax.psum_scatter(
            partial_terms.astype(jnp.bfloat16), "heads", scatter_dimension=1, tiled=True
        )
        .astype(jnp.float32)
        .astype(jnp.bfloat16)
    )


def solution(mesh):
    placed = (
        P("frames", None),
        P(),
        P(None, "heads"),
        P(None, "heads"),
        P(None, "heads"),
        P("heads"),
        P("heads", None),
    )
    return jax.shard_map(
        per_device, mesh=mesh, in_specs=placed, out_specs=P("frames", "heads"), check_vma=False
    )
```

profile of v0, /device:TPU:0, one launch (start us, length us, event | category | flops | bytes accessed | tf_op | source)
XLA Modules:
  0.0 186.0 jit_solution(17141474045914889469)
XLA Ops:
  6.5 1.5 fusion.12
  8.1 3.4 %fusion.15 = bf16[16,4,8,128]{3,2,1,0:T(8,128)(2,1)S(1)} fusion(bf16[4096,512]{1,0:T(8,128)(2,1)} %param.16, bf16[128,4096]{1,0:T(8,128)(2,1)} %param.13, f32[4096]{0:T(1024)} %param.14, f32[128]{0:T(128)S(1)} %add_rsqrt_fusion.1), kind=kOutput, calls=%fused_computation.39 | convolution fusion | flops 539033600 | bytes 5390848 | tf_op jit(solution)/shard_map/dot_general | solution.py:61
  12.2 2.9 %fusion.16 = bf16[16,4,8,128]{3,2,1,0:T(8,128)(2,1)S(1)} fusion(bf16[4096,512]{1,0:T(8,128)(2,1)} %param.17, bf16[128,4096]{1,0:T(8,128)(2,1)S(1)} %copy-done, f32[4096]{0:T(1024)S(1)} %copy-done.2, f32[128]{0:T(128)S(1)} %add_rsqrt_fusion.1), kind=kOutput, calls=%fused_computation.40 | convolution fusion | flops 539033600 | bytes 5390848 | tf_op jit(solution)/shard_map/dot_general | solution.py:62
  15.9 3.0 %convolution_convert_fusion.1 = bf16[128,512]{1,0:T(8,128)(2,1)S(1)} fusion(bf16[4096,512]{1,0:T(8,128)(2,1)} %param.15, bf16[128,4096]{1,0:T(8,128)(2,1)S(1)} %copy-done, f32[4096]{0:T(1024)S(1)} %copy-done.2, f32[128]{0:T(128)S(1)} %add_rsqrt_fusion.1), kind=kOutput, calls=%fused_computation.36 | convolution fusion | flops 539033600 | bytes 5390848 | tf_op jit(solution)/shard_map/dot_general | solution.py:60
  18.9 36.7 %all-gather.3.cloned.1.call-done = bf16[1024,4,128]{2,0,1:T(8,128)(2,1)} async-done(((bf16[128,4,128]{2,0,1:T(8,128)(2,1)}), bf16[1024,4,128]{2,0,1:T(8,128)(2,1)}) %all-gather.3.cloned.1.call-update) | async-done | bytes 1048592 | tf_op jit(solution)/shard_map/all_gather | solution.py:15
  55.6 41.3 %all-gather.5.cloned.1.call-done = bf16[1024,4,128]{2,0,1:T(8,128)(2,1)} async-done(((bf16[128,4,128]{2,0,1:T(8,128)(2,1)}), bf16[1024,4,128]{2,0,1:T(8,128)(2,1)}) %all-gather.5.cloned.1.call-update) | async-done | bytes 1048592 | tf_op jit(solution)/shard_map/all_gather | solution.py:15
  97.0 37.2 %while.23 = (s32[]{:T(128)}, f32[4,64]{1,0:T(4,128)S(1)}, f32[4,64]{1,0:T(4,128)S(1)}, f32[4,64,128]{2,1,0:T(8,128)S(1)}, f32[4,64]{1,0:T(4,128)S(1)}, /*index=5...) while((s32[]{:T(128)}, f32[4,64]{1,0:T(4,128)S(1)}, ...), condition=%wide.region_10.11_spmd, body=%wide.region_1.10_spmd.sunk | while | flops 17179912 | bytes 1640933 | solution.py:99
  98.3 0.9 dynamic-slice_bitcast_fusion.3
  101.7 0.9 dynamic-slice_bitcast_fusion.3
  104.5 0.9 dynamic-slice_bitcast_fusion.3
  106.7 0.9 dynamic-slice_bitcast_fusion.3
  108.9 0.9 dynamic-slice_bitcast_fusion.3
  111.1 0.9 dynamic-slice_bitcast_fusion.3
  113.4 0.9 dynamic-slice_bitcast_fusion.3
  115.6 0.9 dynamic-slice_bitcast_fusion.3
  117.8 0.9 dynamic-slice_bitcast_fusion.3
  120.0 0.9 dynamic-slice_bitcast_fusion.3
  122.2 0.9 dynamic-slice_bitcast_fusion.3
  124.4 0.9 dynamic-slice_bitcast_fusion.3
  126.6 0.9 dynamic-slice_bitcast_fusion.3
  128.8 0.9 dynamic-slice_bitcast_fusion.3
  133.3 0.9 dynamic-slice_bitcast_fusion.3
  135.1 3.9 %convolution_convert_fusion = bf16[128,4096]{1,0:T(8,128)(2,1)} fusion(bf16[128,512]{0,1:T(8,128)(2,1)S(1)} %bitcast.50, bf16[512,4096]{1,0:T(8,128)(2,1)} %param.19), kind=kOutput, calls=%fused_computation.30 | convolution fusion | flops 537395200 | bytes 5373952 | tf_op jit(solution)/shard_map/dot_general | solution.py:127
  139.1 40.4 %reduce-scatter.2.cloned.1.call-done = bf16[128,1024]{1,0:T(8,128)(2,1)} async-done(((bf16[128,4096]{1,0:T(8,128)(2,1)}), bf16[128,1024]{1,0:T(8,128)(2,1)}) %reduce-scatter.2.cloned.1.call-update) | async-done | bytes 262160 | tf_op jit(solution)/shard_map/reduce_scatter | solution.py:129
  (104 shorter events, 16.7 us)
Async XLA Ops:
  6.5 49.1 %all-gather.3.cloned.1.call-start = ((), (), s32[]{:S(2)}) async-start(), calls=%async_computation.1 | async-start | bytes 1179648 | tf_op jit(solution)/shard_map/all_gather | solution.py:15
  8.1 4.2 %copy-start = (bf16[128,4096]{1,0:T(8,128)(2,1)S(1)}, bf16[128,4096]{1,0:T(8,128)(2,1)}, u32[]{:S(2)}) copy-start(bf16[128,4096]{1,0:T(8,128)(2,1)} %param.13) | copy-start | bytes 3145732
  8.1 4.2 %copy-start.2 = (f32[4096]{0:T(1024)S(1)}, f32[4096]{0:T(1024)}, u32[]{:S(2)}) copy-start(f32[4096]{0:T(1024)} %param.14) | copy-start | bytes 49156
  12.2 84.8 %all-gather.5.cloned.1.call-start = ((), (), s32[]{:S(2)}) async-start(), calls=%async_computation.2 | async-start | bytes 1179648 | tf_op jit(solution)/shard_map/all_gather | solution.py:15
  15.9 163.6 %reduce-scatter.2.cloned.1.call-start = ((), (), s32[]{:S(2)}) async-start(), calls=%async_computation.3 | async-start | bytes 1310720 | tf_op jit(solution)/shard_map/reduce_scatter | solution.py:129
  134.2 0.7 copy-start.1
Sparse Core Ops, SparseCore 0:
  12.3 43.2 all-gather.2
  57.8 39.0 all-gather.4
  139.2 40.2 reduce-scatter.1
where the time goes:
time: 187 us; the launch traced here: 186 us
  waiting for transfers between devices  118 us (63%)
  local copies, waits for them, and re-layouts  25.5 us (14%)
  matrix products  14.4 us (8%)
  between operations  13.3 us (7%)
  loops' own time  11.8 us (6%)
  other arithmetic  2.39 us (1%)
    all_gather x2, waiting for transfers between devices, folded(): lax.all_gather(part, axis, axis=dim, tiled=True)  78 us
    reduce_scatter x1, waiting for transfers between devices, per_device(): lax.psum_scatter(partial_terms.astype(jnp.bfloat16), 'heads', scatter_dim...  40.4 us
    squeeze x16, local copies, waits for them, and re-layouts, accumulate(): lax.scan(advance, state_pair, (key_blocks, value_blocks, jnp.arange(block...  14.3 us
    another operation x1, loops' own time, accumulate(): lax.scan(advance, state_pair, (key_blocks, value_blocks, jnp.arange(block...  11.2 us
    dynamic_slice x16, local copies, waits for them, and re-layouts, accumulate(): lax.scan(advance, state_pair, (key_blocks, value_blocks, jnp.arange(block...  9.38 us
    dot_general x1, matrix products, per_device(): partial_terms = jnp.dot(headed, w_out, preferred_element_type=jnp.float32)  3.91 us
  transfers between devices with their start and end apart: 3, of which 3 were waited for; matrix products, arithmetic and copies ran while one was open for 4% of the time, Pallas kernels for 0%

commit v1 on v0

v1 whole, which is shorter than its diff:
```python
import functools
import math

import jax
import jax.numpy as jnp
from jax import lax
from jax.experimental import pallas as pl
from jax.experimental.pallas import tpu as pltpu
from jax.sharding import PartitionSpec as P

HD = 128
EPS = 1e-06
MESH = pl.DeviceIdType.MESH


def fused_kernel(
    n, nh,
    tokens_hbm, norm_gain_ref, wq_hbm, wk_hbm, wv_hbm, head_gain_ref, wo_hbm,
    out_ref,
    tok, normed, wkv, wq, wo, kvout, qout, kv, q, oout, headed, s1, r1, s2, r2, acc,
    tok_sem, w_sem, wo_sem,
    kvs_sem, qs_sem, fw_sem, kvr_sem, qr_sem, os_sem, or_sem,
    s1_sem, r1_sem, s2_sem, r2_sem,
):
    heads = kvout.shape[0]
    rows = tok.shape[0]
    group = n // heads
    half = max(heads // 2, 1)
    me = lax.axis_index("frames")
    lane = lax.axis_index("heads")
    level, member = lax.div(me, group), lax.rem(me, group)
    core, pair = lax.rem(lane, 2), lax.div(lane, 2)
    pairs = nh // 2
    lower = level < half

    def head_at(k):
        return jnp.where(lower, heads - 1 - k, k)

    tok_copy = pltpu.make_async_copy(tokens_hbm, tok, tok_sem)
    tok_copy.start()
    loads = []
    per = 2 if heads % 2 == 0 else 1
    for k in range(heads):
        cols = pl.ds(pl.multiple_of(head_at(k) * HD, HD), HD)
        loads.append((
            pltpu.make_async_copy(wk_hbm.at[:, cols], wkv.at[k, :, pl.ds(0, HD)], w_sem.at[k, 0]),
            pltpu.make_async_copy(wv_hbm.at[:, cols], wkv.at[k, :, pl.ds(HD, HD)], w_sem.at[k, 1]),
            pltpu.make_async_copy(
                wq_hbm.at[:, cols], wq.at[k // per, :, pl.ds((k % per) * HD, HD)], w_sem.at[k, 2]
            ),
        ))
    for first in range(0, heads, per):
        for k in range(first, first + per):
            loads[k][0].start()
            loads[k][1].start()
        for k in range(first, first + per):
            loads[k][2].start()
    wo_copy = pltpu.make_async_copy(wo_hbm, wo, wo_sem)
    wo_copy.start()

    barrier = pltpu.get_barrier_semaphore()
    for d in range(1, heads):
        other = lax.rem(level + d, heads) * group + member
        pl.semaphore_signal(barrier, inc=1, device_id={"frames": other}, device_id_type=MESH)
    for d in range(1, group):
        other = level * group + lax.rem(member + d, group)
        pl.semaphore_signal(barrier, inc=1, device_id={"frames": other}, device_id_type=MESH)
    mate = pair * 2 + 1 - core
    pl.semaphore_signal(barrier, inc=1, device_id={"heads": mate}, device_id_type=MESH)
    for d in range(1, pairs):
        other = lax.rem(pair + d, pairs) * 2 + core
        pl.semaphore_signal(barrier, inc=1, device_id={"heads": other}, device_id_type=MESH)

    tok_copy.wait()
    for start in range(0, rows, 32):
        part = pl.ds(start, 32)
        wide = tok[part, :].astype(jnp.float32)
        scale = lax.rsqrt(jnp.mean(wide * wide, axis=1, keepdims=True) + EPS)
        normed[part, :] = (wide * scale * norm_gain_ref[...]).astype(jnp.bfloat16)

    pl.semaphore_wait(barrier, heads - 1 + group - 1 + 1 + pairs - 1)

    def kv_send(k, target):
        return pltpu.make_async_remote_copy(
            src_ref=kvout.at[k], dst_ref=kv.at[me],
            send_sem=kvs_sem.at[k], recv_sem=kvr_sem.at[me],
            device_id={"frames": target}, device_id_type=MESH,
        )

    def q_send(k, target):
        return pltpu.make_async_remote_copy(
            src_ref=qout.at[k], dst_ref=q.at[level],
            send_sem=qs_sem.at[k], recv_sem=qr_sem.at[level],
            device_id={"frames": target}, device_id_type=MESH,
        )

    def forward(source, d):
        target = level * group + lax.rem(member + d, group)
        return pltpu.make_async_remote_copy(
            src_ref=kv.at[source], dst_ref=kv.at[source],
            send_sem=fw_sem.at[lax.div(source, group), d], recv_sem=kvr_sem.at[source],
            device_id={"frames": target}, device_id_type=MESH,
        )

    def kv_arrived(source):
        return pltpu.make_async_remote_copy(
            src_ref=kv.at[source], dst_ref=kv.at[source],
            send_sem=kvs_sem.at[0], recv_sem=kvr_sem.at[source],
            device_id={"frames": me}, device_id_type=MESH,
        )

    def q_arrived(source):
        return pltpu.make_async_remote_copy(
            src_ref=q.at[source], dst_ref=q.at[source],
            send_sem=qs_sem.at[0], recv_sem=qr_sem.at[source],
            device_id={"frames": me}, device_id_type=MESH,
        )

    for first in range(0, heads, per):
        for k in range(first, first + per):
            loads[k][0].wait()
            loads[k][1].wait()
            block = jnp.dot(normed[...], wkv[k], preferred_element_type=jnp.float32)
            block = block.astype(jnp.bfloat16)
            h = head_at(k)

            @pl.when(h != level)
            def _():
                kvout[k] = block
                kv_send(k, h * group + member).start()

            @pl.when(h == level)
            def _():
                kv[me] = block
                for d in range(1, group):
                    forward(me, d).start()

        for k in range(first, first + per):
            loads[k][2].wait()
        block = jnp.dot(normed[...], wq[first // per], preferred_element_type=jnp.float32)
        block = block.astype(jnp.bfloat16)
        for k in range(first, first + per):
            h = head_at(k)
            part = block[:, (k - first) * HD : (k - first + 1) * HD]

            @pl.when(h != level)
            def _():
                qout[k] = part
                q_send(k, h * group + member).start()

            @pl.when(h == level)
            def _():
                q[level] = part

    for d in range(heads):
        src_level = jnp.where(lower, lax.rem(half + d, heads), lax.rem(half - 1 - d + heads, heads))
        source = src_level * group + member

        @pl.when(src_level != level)
        def _():
            kv_arrived(source).wait_recv()
            for e in range(1, group):
                forward(source, e).start()

    def o_send(i):
        return pltpu.make_async_remote_copy(
            src_ref=oout.at[i],
            dst_ref=headed.at[:, pl.ds(pl.multiple_of(level * HD, HD), HD)],
            send_sem=os_sem.at[i], recv_sem=or_sem.at[level],
            device_id={"frames": i * group + member}, device_id_type=MESH,
        )

    inv_root = 1.0 / math.sqrt(HD)
    gain = head_gain_ref[:, pl.ds(pl.multiple_of(level * HD, HD), HD)]
    for i in range(heads):
        for d in range(1, group):
            kv_arrived(i * group + lax.rem(member + d, group)).wait_recv()

        @pl.when(level != i)
        def _():
            q_arrived(i).wait_recv()

        reach = (i + 1) * group
        keys = kv[:reach, :, :HD].reshape(reach * rows, HD)
        values = kv[:reach, :, HD:].reshape(reach * rows, HD)
        scores = lax.dot_general(
            q[i], keys, (((1,), (1,)), ((), ())), preferred_element_type=jnp.float32
        ) * inv_root
        query_pos = (i * group + member) * rows + lax.broadcasted_iota(jnp.int32, scores.shape, 0)
        key_pos = lax.broadcasted_iota(jnp.int32, scores.shape, 1)
        scores = jnp.where(key_pos <= query_pos, scores, jnp.float32(-1e30))
        top = jnp.max(scores, axis=1, keepdims=True)
        weights = jnp.exp(scores - top)
        total = jnp.sum(weights, axis=1, keepdims=True)
        attended = jnp.dot(
            weights.astype(jnp.bfloat16), values, preferred_element_type=jnp.float32
        ) / total
        scale = lax.rsqrt(jnp.mean(attended * attended, axis=1, keepdims=True) + EPS)
        result = (attended * scale * gain).astype(jnp.bfloat16)

        @pl.when(level != i)
        def _():
            oout[i] = result
            o_send(i).start()

        @pl.when(level == i)
        def _():
            headed[:, pl.ds(pl.multiple_of(level * HD, HD), HD)] = result

    wo_copy.wait()
    for h in range(heads):
        @pl.when(level != h)
        def _():
            here = headed.at[:, pl.ds(h * HD, HD)]
            pltpu.make_async_remote_copy(
                src_ref=here, dst_ref=here, send_sem=os_sem.at[0], recv_sem=or_sem.at[h],
                device_id={"frames": me}, device_id_type=MESH,
            ).wait_recv()

    cw = out_ref.shape[1]
    subs, sw = s1.shape[1], s1.shape[3]
    heads_in = headed[...]

    def partial_at(d, side, s):
        to = lax.rem(pair + d, pairs) * 2 + side
        cols = pl.ds(pl.multiple_of(to * cw + s * sw, sw), sw)
        return jnp.dot(heads_in, wo[:, cols], preferred_element_type=jnp.float32)

    def mate_send(d, s):
        return pltpu.make_async_remote_copy(
            src_ref=s1.at[d, s], dst_ref=r1.at[d, s],
            send_sem=s1_sem.at[d, s], recv_sem=r1_sem.at[d, s],
            device_id={"heads": mate}, device_id_type=MESH,
        )

    def pair_send(d, s):
        return pltpu.make_async_remote_copy(
            src_ref=s2.at[d - 1, s], dst_ref=r2.at[d - 1, s],
            send_sem=s2_sem.at[d - 1, s], recv_sem=r2_sem.at[d - 1, s],
            device_id={"heads": lax.rem(pair + d, pairs) * 2 + core}, device_id_type=MESH,
        )

    order = [(d % pairs, s) for d in range(1, pairs + 1) for s in range(subs)]
    for d, s in order:
        s1[d, s] = partial_at(d, 1 - core, s).astype(jnp.bfloat16)
        mate_send(d, s).start()
    for d, s in order:
        own = partial_at(d, core, s)
        mate_send(d, s).wait_recv()
        own = own + r1[d, s].astype(jnp.float32)
        if d:
            s2[d - 1, s] = own.astype(jnp.bfloat16)
            pair_send(d, s).start()
        else:
            acc[s] = own
    for s in range(subs):
        whole = acc[s]
        for d in range(1, pairs):
            pair_send(d, s).wait_recv()
            whole = whole + r2[d - 1, s].astype(jnp.float32)
        out_ref[:, s * sw : (s + 1) * sw] = whole.astype(jnp.bfloat16)

    for d, s in order:
        mate_send(d, s).wait_send()
        if d:
            pair_send(d, s).wait_send()
    for i in range(heads):
        @pl.when(level != i)
        def _():
            o_send(i).wait_send()

        for d in range(1, group):
            forward(i * group + member, d).wait_send()
    for k in range(heads):
        @pl.when(head_at(k) != level)
        def _():
            kv_send(k, head_at(k) * group + member).wait_send()
            q_send(k, head_at(k) * group + member).wait_send()


def solution(mesh):
    n, nh = mesh.shape["frames"], mesh.shape["heads"]

    def per_device(tokens, norm_gain, w_query, w_key, w_value, head_gain, w_out):
        rows, depth = tokens.shape
        heads = w_query.shape[1] // HD
        width = w_out.shape[1]
        cw = width // nh
        subs = 2
        sw = cw // subs
        pairs = nh // 2
        group = n // heads
        per = 2 if heads % 2 == 0 else 1
        bf = jnp.bfloat16
        dma = pltpu.SemaphoreType.DMA
        hbm = pl.BlockSpec(memory_space=pltpu.HBM)
        vmem = pl.BlockSpec(memory_space=pltpu.VMEM)
        return pl.pallas_call(
            functools.partial(fused_kernel, n, nh),
            out_shape=jax.ShapeDtypeStruct((rows, cw), bf),
            in_specs=[hbm, vmem, hbm, hbm, hbm, vmem, hbm],
            out_specs=vmem,
            scratch_shapes=[
                pltpu.VMEM((rows, depth), bf),
                pltpu.VMEM((rows, depth), bf),
                pltpu.VMEM((heads, depth, 2 * HD), bf),
                pltpu.VMEM((heads // per, depth, per * HD), bf),
                pltpu.VMEM(w_out.shape, bf),
                pltpu.VMEM((heads, rows, 2 * HD), bf),
                pltpu.VMEM((heads, rows, HD), bf),
                pltpu.VMEM((n, rows, 2 * HD), bf),
                pltpu.VMEM((heads, rows, HD), bf),
                pltpu.VMEM((heads, rows, HD), bf),
                pltpu.VMEM((rows, heads * HD), bf),
                pltpu.VMEM((pairs, subs, rows, sw), bf),
                pltpu.VMEM((pairs, subs, rows, sw), bf),
                pltpu.VMEM((pairs - 1, subs, rows, sw), bf),
                pltpu.VMEM((pairs - 1, subs, rows, sw), bf),
                pltpu.VMEM((subs, rows, sw), jnp.float32),
                dma,
                dma((heads, 3)),
                dma,
                dma((heads,)),
                dma((heads,)),
                dma((heads, group)),
                dma((n,)),
                dma((heads,)),
                dma((heads,)),
                dma((heads,)),
                dma((pairs, subs)),
                dma((pairs, subs)),
                dma((pairs - 1, subs)),
                dma((pairs - 1, subs)),
            ],
            compiler_params=pltpu.CompilerParams(
                collective_id=0, has_side_effects=True, vmem_limit_bytes=60 * 1024 * 1024
            ),
            name="fused_block",
        )(tokens, norm_gain[None, :], w_query, w_key, w_value, head_gain[None, :], w_out)

    placed = (
        P("frames", None),
        P(),
        P(None, "heads"),
        P(None, "heads"),
        P(None, "heads"),
        P("heads"),
        P("heads", None),
    )
    return jax.shard_map(
        per_device, mesh=mesh, in_specs=placed, out_specs=P("frames", "heads"), check_vma=False
    )
```

time: 187 us -> 40.6 us (0.22)
  waiting for transfers between devices: 118 us -> 0 us
  Pallas kernels: 0 us -> 38.7 us
  local copies, waits for them, and re-layouts: 25.5 us -> 1.67 us
  matrix products: 14.4 us -> 0 us
  between operations: 13.3 us -> 0.01 us
  loops' own time: 11.8 us -> 0 us
  other arithmetic: 2.39 us -> 0 us
    all_gather x2 -> x0, waiting for transfers between devices: 78 us -> none  [folded(): lax.all_gather(part, axis, axis=dim, tiled=True)]
    reduce_scatter x1 -> x0, waiting for transfers between devices: 40.4 us -> none  [per_device(): lax.psum_scatter(partial_terms.astype(jnp.bfloat16), 'heads', scatter_dim...]
    pallas_call x0 -> x1, Pallas kernels: none -> 38.7 us  [per_device(): pl.pallas_call(functools.partial(fused_kernel, n, nh), out_shape=jax.Shap...]
    dot_general x10 -> x0, matrix products: 14.4 us -> none  [the longest x1 3.91 us: per_device(): partial_terms = jnp.dot(headed, w_out, preferred_element_type=jnp.float32)]
    squeeze x16 -> x0, local copies, waits for them, and re-layouts: 14.3 us -> none  [accumulate(): lax.scan(advance, state_pair, (key_blocks, value_blocks, jnp.arange(block...]
    another operation x33 -> x0, loops' own time: 11.8 us -> none  [the longest x1 11.2 us: accumulate(): lax.scan(advance, state_pair, (key_blocks, value_blocks, jnp.arange(block...]
    dynamic_slice x16 -> x0, local copies, waits for them, and re-layouts: 9.38 us -> none  [accumulate(): lax.scan(advance, state_pair, (key_blocks, value_blocks, jnp.arange(block...]
  transfers between devices with their start and end apart: 3 -> 0, of which waited for: 3 -> 0; matrix products, arithmetic and copies ran while one was open for 4% -> 0% of each run, Pallas kernels for 0% -> 0%
where the time goes in v1:
time: 40.6 us; the launch traced here: 40.4 us
  Pallas kernels  38.7 us (95%)
  local copies, waits for them, and re-layouts  1.67 us (4%)
    pallas_call x1, Pallas kernels, per_device(): pl.pallas_call(functools.partial(fused_kernel, n, nh), out_shape=jax.Shap...  38.7 us
    unnamed x1, local copies, waits for them, and re-layouts  1.67 us

profile of v1, /device:TPU:0, one launch (start us, length us, event | category | flops | bytes accessed | tf_op | source)
XLA Modules:
  0.0 40.4 jit_solution(10196106608453645863)
XLA Ops:
  0.0 38.7 %fused_block.1 = bf16[128,1024]{1,0:T(8,128)(2,1)} custom-call(bf16[128,4096]{1,0:T(8,128)(2,1)} %tokens_hbm.1, f32[1,4096]{1,0:T(1,128)} %bitcast.2, bf16[4096,512]{1,0:T(8,128)(2,1)} %wq_hbm.1, bf16[4096,512]{1,0:T(8,128)(2,1)} %wk_hbm.1, bf16[4096,512]{1,0:T(8,128)(2,1)} %wv_hbm.1, f32[1,512]{1,0:T(1,128)} %bitcast.3, bf16[512,4096]{1,0:T(8,128)(2,1)} %wo_hbm.1), custom_call_target="tpu_custom_call" | custom-call | tf_op jit(solution)/shard_map/fused_block/pallas_call | solution.py:298
  38.7 1.7 %copy.9 = bf16[128,1024]{1,0:T(8,128)(2,1)} copy(bf16[128,1024]{1,0:T(8,128)(2,1)} %fused_block.1) | data formatting | bytes 524288

commit v2 on v1

--- a/solution.py
+++ b/solution.py
@@ -49,14 +49,8 @@
                 wq_hbm.at[:, cols], wq.at[k // per, :, pl.ds((k % per) * HD, HD)], w_sem.at[k, 2]
             ),
         ))
-    for first in range(0, heads, per):
-        for k in range(first, first + per):
-            loads[k][0].start()
-            loads[k][1].start()
-        for k in range(first, first + per):
-            loads[k][2].start()
-    wo_copy = pltpu.make_async_copy(wo_hbm, wo, wo_sem)
-    wo_copy.start()
+    loads[0][0].start()
+    loads[0][1].start()
 
     barrier = pltpu.get_barrier_semaphore()
     for d in range(1, heads):
@@ -72,6 +66,13 @@
         pl.semaphore_signal(barrier, inc=1, device_id={"heads": other}, device_id_type=MESH)
 
     tok_copy.wait()
+    for k in range(1, heads):
+        loads[k][0].start()
+        loads[k][1].start()
+    for k in range(heads):
+        loads[k][2].start()
+    wo_copy = pltpu.make_async_copy(wo_hbm, wo, wo_sem)
+    wo_copy.start()
     for start in range(0, rows, 32):
         part = pl.ds(start, 32)
         wide = tok[part, :].astype(jnp.float32)
@@ -116,25 +117,25 @@
             device_id={"frames": me}, device_id_type=MESH,
         )
 
+    for k in range(heads):
+        loads[k][0].wait()
+        loads[k][1].wait()
+        block = jnp.dot(normed[...], wkv[k], preferred_element_type=jnp.float32)
+        block = block.astype(jnp.bfloat16)
+        h = head_at(k)
+
+        @pl.when(h != level)
+        def _():
+            kvout[k] = block
+            kv_send(k, h * group + member).start()
+
+        @pl.when(h == level)
+        def _():
+            kv[me] = block
+            for d in range(1, group):
+                forward(me, d).start()
+
     for first in range(0, heads, per):
-        for k in range(first, first + per):
-            loads[k][0].wait()
-            loads[k][1].wait()
-            block = jnp.dot(normed[...], wkv[k], preferred_element_type=jnp.float32)
-            block = block.astype(jnp.bfloat16)
-            h = head_at(k)
-
-            @pl.when(h != level)
-            def _():
-                kvout[k] = block
-                kv_send(k, h * group + member).start()
-
-            @pl.when(h == level)
-            def _():
-                kv[me] = block
-                for d in range(1, group):
-                    forward(me, d).start()
-
         for k in range(first, first + per):
             loads[k][2].wait()
         block = jnp.dot(normed[...], wq[first // per], preferred_element_type=jnp.float32)
@@ -152,8 +153,13 @@
             def _():
                 q[level] = part
 
+    inner = (level == half) | (level == half - 1)
+    turn = jnp.where(inner, half, 0)
     for d in range(heads):
-        src_level = jnp.where(lower, lax.rem(half + d, heads), lax.rem(half - 1 - d + heads, heads))
+        step = lax.rem(turn + d, heads)
+        src_level = jnp.where(
+            lower, lax.rem(half + step, heads), lax.rem(half - 1 - step + heads, heads)
+        )
         source = src_level * group + member
 
         @pl.when(src_level != level)
@@ -241,18 +247,20 @@
         )
 
     order = [(d % pairs, s) for d in range(1, pairs + 1) for s in range(subs)]
-    for d, s in order:
-        s1[d, s] = partial_at(d, 1 - core, s).astype(jnp.bfloat16)
-        mate_send(d, s).start()
-    for d, s in order:
-        own = partial_at(d, core, s)
-        mate_send(d, s).wait_recv()
-        own = own + r1[d, s].astype(jnp.float32)
-        if d:
-            s2[d - 1, s] = own.astype(jnp.bfloat16)
-            pair_send(d, s).start()
-        else:
-            acc[s] = own
+    for to in range(1, pairs + 1):
+        d = to % pairs
+        for s in range(subs):
+            s1[d, s] = partial_at(d, 1 - core, s).astype(jnp.bfloat16)
+            mate_send(d, s).start()
+        for s in range(subs):
+            own = partial_at(d, core, s)
+            mate_send(d, s).wait_recv()
+            own = own + r1[d, s].astype(jnp.float32)
+            if d:
+                s2[d - 1, s] = own.astype(jnp.bfloat16)
+                pair_send(d, s).start()
+            else:
+                acc[s] = own
     for s in range(subs):
         whole = acc[s]
         for d in range(1, pairs):
@@ -286,7 +294,7 @@
         heads = w_query.shape[1] // HD
         width = w_out.shape[1]
         cw = width // nh
-        subs = 2
+        subs = 4
         sw = cw // subs
         pairs = nh // 2
         group = n // heads

time: 40.6 us -> 36.5 us (0.90)
  Pallas kernels: 38.7 us -> 34.6 us
    pallas_call x1, Pallas kernels: 38.7 us -> 34.6 us  [per_device(): pl.pallas_call(functools.partial(fused_kernel, n, nh), out_shape=jax.Shap...]
where the time goes in v2:
time: 36.5 us; the launch traced here: 36.3 us
  Pallas kernels  34.6 us (95%)
  local copies, waits for them, and re-layouts  1.67 us (5%)
    pallas_call x1, Pallas kernels, per_device(): pl.pallas_call(functools.partial(fused_kernel, n, nh), out_shape=jax.Shap...  34.6 us
    unnamed x1, local copies, waits for them, and re-layouts  1.67 us

profile of v2, /device:TPU:0, one launch (start us, length us, event | category | flops | bytes accessed | tf_op | source)
XLA Modules:
  0.0 36.3 jit_solution(18306875794725406624)
XLA Ops:
  0.0 34.6 %fused_block.1 = bf16[128,1024]{1,0:T(8,128)(2,1)} custom-call(bf16[128,4096]{1,0:T(8,128)(2,1)} %tokens_hbm.1, f32[1,4096]{1,0:T(1,128)} %bitcast.2, bf16[4096,512]{1,0:T(8,128)(2,1)} %wq_hbm.1, bf16[4096,512]{1,0:T(8,128)(2,1)} %wk_hbm.1, bf16[4096,512]{1,0:T(8,128)(2,1)} %wv_hbm.1, f32[1,512]{1,0:T(1,128)} %bitcast.3, bf16[512,4096]{1,0:T(8,128)(2,1)} %wo_hbm.1), custom_call_target="tpu_custom_call" | custom-call | tf_op jit(solution)/shard_map/fused_block/pallas_call | solution.py:306
  34.6 1.7 %copy.9 = bf16[128,1024]{1,0:T(8,128)(2,1)} copy(bf16[128,1024]{1,0:T(8,128)(2,1)} %fused_block.1) | data formatting | bytes 524288

commit v3 on v2

--- a/solution.py
+++ b/solution.py
@@ -341,7 +341,7 @@
                 dma((pairs - 1, subs)),
             ],
             compiler_params=pltpu.CompilerParams(
-                collective_id=0, has_side_effects=True, vmem_limit_bytes=60 * 1024 * 1024
+                collective_id=0, has_side_effects=True, vmem_limit_bytes=55783424
             ),
             name="fused_block",
         )(tokens, norm_gain[None, :], w_query, w_key, w_value, head_gain[None, :], w_out)

time: 36.5 us -> 35.5 us (0.973)
  Pallas kernels: 34.6 us -> 33.2 us
  local copies, waits for them, and re-layouts: 1.67 us -> 2.1 us
    pallas_call x1, Pallas kernels: 34.6 us -> 33.2 us  [per_device(): pl.pallas_call(functools.partial(fused_kernel, n, nh), out_shape=jax.Shap...]
    unnamed x1 -> x5, local copies, waits for them, and re-layouts: 1.67 us -> 2.1 us
where the time goes in v3:
time: 35.5 us; the launch traced here: 35.3 us
  Pallas kernels  33.2 us (94%)
  local copies, waits for them, and re-layouts  2.1 us (6%)
    pallas_call x1, Pallas kernels, per_device(): pl.pallas_call(functools.partial(fused_kernel, n, nh), out_shape=jax.Shap...  33.2 us
    unnamed x5, local copies, waits for them, and re-layouts  2.1 us

profile of v3, /device:TPU:0, one launch (start us, length us, event | category | flops | bytes accessed | tf_op | source)
XLA Modules:
  0.0 35.3 jit_solution(8279724319763197412)
XLA Ops:
  0.0 0.0 copy-start
  0.0 0.7 %copy-done = f32[4096]{0:T(1024)S(1)} copy-done((f32[4096]{0:T(1024)S(1)}, f32[4096]{0:T(1024)}, u32[]{:S(2)}) %copy-start) | copy-done | bytes 16408
  0.7 0.0 copy-start.1
  0.7 0.7 %copy-done.1 = f32[512]{0:T(512)S(1)} copy-done((f32[512]{0:T(512)S(1)}, f32[512]{0:T(512)}, u32[]{:S(2)}) %copy-start.1) | copy-done | bytes 2072
  1.4 33.2 %fused_block.1 = bf16[128,1024]{1,0:T(8,128)(2,1)S(1)} custom-call(bf16[128,4096]{1,0:T(8,128)(2,1)} %tokens_hbm.1, f32[1,4096]{1,0:T(1,128)S(1)} %bitcast.2, bf16[4096,512]{1,0:T(8,128)(2,1)} %wq_hbm.1, bf16[4096,512]{1,0:T(8,128)(2,1)} %wk_hbm.1, bf16[4096,512]{1,0:T(8,128)(2,1)} %wv_hbm.1, f32[1,512]{1,0:T(1,128)S(1)} %bitcast.3, bf16[512,4096]{1,0:T(8,128)(2,1)} %wo_hbm.1), custom_call_target="tpu_custom_call" | custom-call | tf_op jit(solution)/shard_map/fused_block/pallas_call | solution.py:306
  34.6 0.7 %copy.9 = bf16[128,1024]{1,0:T(8,128)(2,1)} copy(bf16[128,1024]{1,0:T(8,128)(2,1)S(1)} %fused_block.1) | data formatting | bytes 524288
Async XLA Ops:
  0.0 0.7 %copy-start = (f32[4096]{0:T(1024)S(1)}, f32[4096]{0:T(1024)}, u32[]{:S(2)}) copy-start(f32[4096]{0:T(1024)} %param.8) | copy-start | bytes 49156
  0.7 0.7 %copy-start.1 = (f32[512]{0:T(512)S(1)}, f32[512]{0:T(512)}, u32[]{:S(2)}) copy-start(f32[512]{0:T(512)} %param.12) | copy-start | bytes 6148

commit v4 on v3

--- a/solution.py
+++ b/solution.py
@@ -294,7 +294,7 @@
         heads = w_query.shape[1] // HD
         width = w_out.shape[1]
         cw = width // nh
-        subs = 4
+        subs = 1
         sw = cw // subs
         pairs = nh // 2
         group = n // heads

time: 35.5 us -> 34.4 us (0.969)
  Pallas kernels: 33.2 us -> 31.9 us
    pallas_call x1, Pallas kernels: 33.2 us -> 31.9 us  [per_device(): pl.pallas_call(functools.partial(fused_kernel, n, nh), out_shape=jax.Shap...]
where the time goes in v4:
time: 34.4 us; the launch traced here: 34.1 us
  Pallas kernels  31.9 us (93%)
  local copies, waits for them, and re-layouts  2.1 us (6%)
    pallas_call x1, Pallas kernels, per_device(): pl.pallas_call(functools.partial(fused_kernel, n, nh), out_shape=jax.Shap...  31.9 us
    unnamed x5, local copies, waits for them, and re-layouts  2.1 us

profile of v4, /device:TPU:0, one launch (start us, length us, event | category | flops | bytes accessed | tf_op | source)
XLA Modules:
  0.0 34.1 jit_solution(2578602256637054701)
XLA Ops:
  0.0 0.0 copy-start
  0.0 0.7 %copy-done = f32[4096]{0:T(1024)S(1)} copy-done((f32[4096]{0:T(1024)S(1)}, f32[4096]{0:T(1024)}, u32[]{:S(2)}) %copy-start) | copy-done | bytes 16408
  0.7 0.0 copy-start.1
  0.7 0.7 %copy-done.1 = f32[512]{0:T(512)S(1)} copy-done((f32[512]{0:T(512)S(1)}, f32[512]{0:T(512)}, u32[]{:S(2)}) %copy-start.1) | copy-done | bytes 2072
  1.4 31.9 %fused_block.1 = bf16[128,1024]{1,0:T(8,128)(2,1)S(1)} custom-call(bf16[128,4096]{1,0:T(8,128)(2,1)} %tokens_hbm.1, f32[1,4096]{1,0:T(1,128)S(1)} %bitcast.2, bf16[4096,512]{1,0:T(8,128)(2,1)} %wq_hbm.1, bf16[4096,512]{1,0:T(8,128)(2,1)} %wk_hbm.1, bf16[4096,512]{1,0:T(8,128)(2,1)} %wv_hbm.1, f32[1,512]{1,0:T(1,128)S(1)} %bitcast.3, bf16[512,4096]{1,0:T(8,128)(2,1)} %wo_hbm.1), custom_call_target="tpu_custom_call" | custom-call | tf_op jit(solution)/shard_map/fused_block/pallas_call | solution.py:306
  33.4 0.7 %copy.9 = bf16[128,1024]{1,0:T(8,128)(2,1)} copy(bf16[128,1024]{1,0:T(8,128)(2,1)S(1)} %fused_block.1) | data formatting | bytes 524288
Async XLA Ops:
  0.0 0.7 %copy-start = (f32[4096]{0:T(1024)S(1)}, f32[4096]{0:T(1024)}, u32[]{:S(2)}) copy-start(f32[4096]{0:T(1024)} %param.8) | copy-start | bytes 49156
  0.7 0.7 %copy-start.1 = (f32[512]{0:T(512)S(1)}, f32[512]{0:T(512)}, u32[]{:S(2)}) copy-start(f32[512]{0:T(512)} %param.12) | copy-start | bytes 6148
